TPU v7x, 32 devices: a whole 2x2x4 slice. The times are simulated.
32 devices in a mesh: dp: 16 (over z, y, core), tensor: 2 (over x).
Axes of the slice: x: 2, y: 2, z: 4, core: 2. Of those that a mesh axis runs over, the one named last changes fastest.
Arguments:
- tokens: bfloat16 [21760, 1024], P('dp'), may hold values from -6 to 6
- d_out: bfloat16 [21760, 1024], P('dp'), may hold values from -6 to 6
- labels: int32 [32], replicated, may hold values from 0 to 999
- scale_ids: int32 [32, 680], P('dp'), may hold values from 0 to 9, never falling along the last dimension, each value on 1 to 256 neighbouring positions
- class_table: bfloat16 [1000, 1024], P(None, 'tensor'), may hold values from -6 to 6
- ada_weight: bfloat16 [1024, 6144], P(None, 'tensor'), may hold values from -0.1875 to 0.1875
- ada_bias: bfloat16 [6144], P('tensor'), may hold values from -3 to 3
- qkv_weight: bfloat16 [1024, 3, 1024], P(None, None, 'tensor'), may hold values from -0.1875 to 0.1875
- q_bias: bfloat16 [1024], P('tensor'), may hold values from -3 to 3
- v_bias: bfloat16 [1024], P('tensor'), may hold values from -3 to 3
- qk_scale: float32 [16], P('tensor'), may hold values from 2.3 to 3
- proj_weight: bfloat16 [1024, 1024], P('tensor'), may hold values from -0.75 to 0.75
- proj_bias: bfloat16 [1024], replicated, may hold values from -2 to 2
- fc1_weight: bfloat16 [1024, 4096], P(None, 'tensor'), may hold values from -0.1875 to 0.1875
- fc1_bias: bfloat16 [4096], P('tensor'), may hold values from -2 to 2
- fc2_weight: bfloat16 [4096, 1024], P('tensor'), may hold values from -0.1875 to 0.1875
- fc2_bias: bfloat16 [1024], replicated, may hold values from -2 to 2
Outputs:
- out: bfloat16 [21760, 1024], P('dp')
- d_tokens: bfloat16 [21760, 1024], P('dp')
- grad_table: float32 [1000, 1024], P(None, 'tensor')
- grad_ada: float32 [1024, 6144], P(None, 'tensor')
- grad_ada_bias: float32 [6144], P('tensor')
- grad_qkv: float32 [1024, 3, 1024], P(None, None, 'tensor')
- grad_q_bias: float32 [1024], P('tensor')
- grad_v_bias: float32 [1024], P('tensor')
- grad_qk_scale: float32 [16], P('tensor')
- grad_proj: float32 [1024, 1024], P('tensor')
- grad_proj_bias: float32 [1024], replicated
- grad_fc1: float32 [1024, 4096], P(None, 'tensor')
- grad_fc1_bias: float32 [4096], P('tensor')
- grad_fc2: float32 [4096, 1024], P('tensor')
- grad_fc2_bias: float32 [1024], replicated
Inputs may be any that keep to these rules, and one draw needn't show every extreme that they name: `scale_ids`: in each image the scale indices never fall, each of the 10 scales holds 1 to 256 tokens, and some scale of every image holds exactly 256.
All inputs are finite; a program needn't handle non-finite values.
Results may differ from a plain program's by a relative error of at most 0.033.
Values may be sent and summed in bfloat16 or wider, within the bound.
A program may use at most 320 MiB of HBM per device.

v0:
```python
from functools import partial
import jax
import jax.numpy as jnp
from jax import lax
from jax.sharding import PartitionSpec as P

epsilon = 1e-06
highest = lax.Precision.HIGHEST


def tensor_sum(part):
    if lax.axis_size("tensor") == 2:
        other = lax.ppermute(part, "tensor", [(0, 1), (1, 0)])
        return part.astype(jnp.float32) + other.astype(jnp.float32)
    return lax.psum(part, "tensor").astype(jnp.float32)


def layer_stats(values):
    center = values - jnp.mean(values, axis=-1, keepdims=True)
    inv_std = lax.rsqrt(jnp.mean(center * center, axis=-1, keepdims=True) + epsilon)
    return (center * inv_std, inv_std)


def layer_back(d_normed, normed, inv_std):
    first_mean = jnp.mean(d_normed, axis=-1, keepdims=True)
    second_mean = jnp.mean(d_normed * normed, axis=-1, keepdims=True)
    return inv_std * (d_normed - first_mean - normed * second_mean)


def per_device(
    tokens,
    d_out,
    labels,
    scale_ids,
    class_table,
    ada_weight,
    ada_bias,
    qkv_weight,
    q_bias,
    v_bias,
    qk_scale,
    proj_weight,
    proj_bias,
    fc1_weight,
    fc1_bias,
    fc2_weight,
    fc2_bias,
):
    f32 = jnp.float32
    bf16 = jnp.bfloat16
    images = scale_ids.shape[0]
    length = scale_ids.shape[1]
    model_width = tokens.shape[1]
    rows_all = images * length
    classes = class_table.shape[0]
    heads_here = qk_scale.shape[0]
    local_width = qkv_weight.shape[2]
    head_size = local_width // heads_here
    mod_width = ada_weight.shape[1]
    first_image = lax.axis_index("dp") * images
    class_ids = jnp.arange(classes, dtype=jnp.int32)
    pick_all = labels[:, None] == class_ids[None, :]
    cond_all_cols = jnp.dot(pick_all.astype(bf16), class_table, preferred_element_type=f32)
    cond_all = lax.all_gather(cond_all_cols.astype(bf16), "tensor", axis=1, tiled=True)
    cond_full = lax.dynamic_slice_in_dim(cond_all, first_image, images)
    act_cond = jax.nn.silu(cond_full.astype(f32)).astype(bf16)
    mod_cols = jnp.dot(act_cond, ada_weight, preferred_element_type=f32) + ada_bias.astype(f32)
    modul = lax.all_gather(mod_cols, "tensor", axis=1, tiled=True)
    gain_one, gain_two, scale_one, scale_two, shift_one, shift_two = [
        modul[:, None, member * model_width : (member + 1) * model_width] for member in range(6)
    ]
    inputs = tokens.astype(f32).reshape(images, length, model_width)
    normed_one, inv_std_one = layer_stats(inputs)
    hidden_one = (
        (normed_one * (1.0 + scale_one) + shift_one).astype(bf16).reshape(rows_all, model_width)
    )
    bias_stack = jnp.stack([q_bias.astype(f32), jnp.zeros(q_bias.shape, f32), v_bias.astype(f32)])
    qkv_val = (
        jnp.einsum("rd,dpc->rpc", hidden_one, qkv_weight, preferred_element_type=f32)
        + bias_stack[None]
    )
    qkv_val = qkv_val.reshape(images, length, 3, heads_here, head_size)
    query_raw = qkv_val[:, :, 0]
    key_raw = qkv_val[:, :, 1]
    value_raw = qkv_val[:, :, 2]
    query_inv = lax.rsqrt(jnp.sum(query_raw * query_raw, axis=-1, keepdims=True) + epsilon)
    query_unit = query_raw * query_inv
    growth = jnp.exp(qk_scale)[None, None, :, None]
    query_scaled = query_unit * growth
    query_low = query_scaled.astype(bf16)
    key_inv = lax.rsqrt(jnp.sum(key_raw * key_raw, axis=-1, keepdims=True) + epsilon)
    key_unit = key_raw * key_inv
    key_low = key_unit.astype(bf16)
    value_low = value_raw.astype(bf16)
    allowed = scale_ids[:, None, None, :] <= scale_ids[:, None, :, None]

    def masked_scores():
        scores = jnp.einsum("ishe,ithe->ihst", query_low, key_low, preferred_element_type=f32)
        return jnp.where(allowed, scores, f32(-1e30))

    masked = masked_scores()
    row_max = jnp.max(masked, axis=-1, keepdims=True)
    weights_exp = jnp.exp(masked - row_max)
    row_total = jnp.sum(weights_exp, axis=-1, keepdims=True)
    log_total = row_max + jnp.log(row_total)
    probs_low = (weights_exp / row_total).astype(bf16)
    attn_out = (
        jnp.einsum("ihst,ithe->ishe", probs_low, value_low, preferred_element_type=f32)
        .reshape(rows_all, local_width)
        .astype(bf16)
    )
    gelu_tanh = partial(jax.nn.gelu, approximate=True)
    d_result = d_out.astype(f32).reshape(images, length, model_width)
    branch_one = tensor_sum(jnp.dot(attn_out, proj_weight, preferred_element_type=f32).astype(bf16))
    branch_one = (branch_one + proj_bias.astype(f32)).reshape(images, length, model_width)
    middle = inputs + gain_one * branch_one
    normed_two, inv_std_two = layer_stats(middle)
    hidden_two = (
        (normed_two * (1.0 + scale_two) + shift_two).astype(bf16).reshape(rows_all, model_width)
    )
    pre_act = jnp.dot(hidden_two, fc1_weight, preferred_element_type=f32) + fc1_bias.astype(f32)
    mlp_low = gelu_tanh(pre_act).astype(bf16)
    branch_two = tensor_sum(jnp.dot(mlp_low, fc2_weight, preferred_element_type=f32).astype(bf16))
    branch_two = (branch_two + fc2_bias.astype(f32)).reshape(images, length, model_width)
    result = (middle + gain_two * branch_two).astype(bf16).reshape(rows_all, model_width)
    d_branch_two = (gain_two * d_result).astype(bf16).reshape(rows_all, model_width)
    grad_fc2 = jnp.einsum("rf,rd->fd", mlp_low, d_branch_two, preferred_element_type=f32)
    grad_fc2_bias = jnp.sum(d_branch_two.astype(f32), axis=0)
    d_mlp = jnp.einsum("rd,fd->rf", d_branch_two, fc2_weight, preferred_element_type=f32)
    gelu_value, gelu_pull = jax.vjp(gelu_tanh, pre_act)
    d_pre = gelu_pull(d_mlp)[0].astype(bf16)
    grad_fc1 = jnp.einsum("rd,rf->df", hidden_two, d_pre, preferred_element_type=f32)
    grad_fc1_bias = jnp.sum(d_pre.astype(f32), axis=0)
    d_hidden_two = tensor_sum(
        jnp.einsum("rf,df->rd", d_pre, fc1_weight, preferred_element_type=f32).astype(bf16)
    )
    d_hidden_two = d_hidden_two.reshape(images, length, model_width)
    d_middle = d_result + layer_back(d_hidden_two * (1.0 + scale_two), normed_two, inv_std_two)
    d_branch_one = (gain_one * d_middle).astype(bf16).reshape(rows_all, model_width)
    grad_proj = jnp.einsum("rc,rd->cd", attn_out, d_branch_one, preferred_element_type=f32)
    grad_proj_bias = jnp.sum(d_branch_one.astype(f32), axis=0)
    d_attn = jnp.einsum("rd,cd->rc", d_branch_one, proj_weight, preferred_element_type=f32).astype(
        bf16
    )
    d_attn = d_attn.reshape(images, length, heads_here, head_size)
    again_probs = jnp.exp(masked_scores() - log_total)
    again_low = again_probs.astype(bf16)
    d_probs = jnp.einsum("ishe,ithe->ihst", d_attn, value_low, preferred_element_type=f32)
    d_scores = (
        again_probs * (d_probs - jnp.sum(again_probs * d_probs, axis=-1, keepdims=True))
    ).astype(bf16)
    d_query_scaled = jnp.einsum("ihst,ithe->ishe", d_scores, key_low, preferred_element_type=f32)
    d_key_unit = jnp.einsum("ihst,ishe->ithe", d_scores, query_low, preferred_element_type=f32)
    d_value = jnp.einsum("ihst,ishe->ithe", again_low, d_attn, preferred_element_type=f32)
    grad_scale = jnp.sum(d_query_scaled * query_scaled, axis=(0, 1, 3))
    d_query_unit = d_query_scaled * growth
    d_query = query_inv * (
        d_query_unit - query_unit * jnp.sum(d_query_unit * query_unit, axis=-1, keepdims=True)
    )
    d_key = key_inv * (
        d_key_unit - key_unit * jnp.sum(d_key_unit * key_unit, axis=-1, keepdims=True)
    )
    d_qkv = (
        jnp.stack([d_query, d_key, d_value], axis=2).reshape(rows_all, 3, local_width).astype(bf16)
    )
    grad_q_bias = jnp.sum(d_qkv[:, 0].astype(f32), axis=0)
    grad_v_bias = jnp.sum(d_qkv[:, 2].astype(f32), axis=0)
    grad_qkv = jnp.einsum("rd,rpc->dpc", hidden_one, d_qkv, preferred_element_type=f32)
    d_hidden_one = tensor_sum(
        jnp.einsum("rpc,dpc->rd", d_qkv, qkv_weight, preferred_element_type=f32).astype(bf16)
    )
    d_hidden_one = d_hidden_one.reshape(images, length, model_width)
    d_inputs = d_middle + layer_back(d_hidden_one * (1.0 + scale_one), normed_one, inv_std_one)
    d_tokens = d_inputs.astype(bf16).reshape(rows_all, model_width)
    d_modul = jnp.concatenate(
        [
            jnp.sum(d_middle * branch_one, axis=1),
            jnp.sum(d_result * branch_two, axis=1),
            jnp.sum(d_hidden_one * normed_one, axis=1),
            jnp.sum(d_hidden_two * normed_two, axis=1),
            jnp.sum(d_hidden_one, axis=1),
            jnp.sum(d_hidden_two, axis=1),
        ],
        axis=1,
    ).astype(bf16)
    col_start = lax.axis_index("tensor") * mod_width
    dmod_cols = lax.dynamic_slice_in_dim(d_modul, col_start, mod_width, 1)
    dmod_all = lax.all_gather(dmod_cols, "dp", axis=0, tiled=True)
    small = [grad_q_bias, grad_v_bias, grad_scale, grad_proj_bias, grad_fc1_bias, grad_fc2_bias]
    sizes = [item.shape[0] for item in small]
    packed = lax.all_gather(jnp.concatenate(small), "dp", axis=0, tiled=False)
    packed = jnp.sum(packed, axis=0)
    ends = [sum(sizes[: k + 1]) for k in range(len(sizes))]
    grad_q_bias, grad_v_bias, grad_scale, grad_proj_bias, grad_fc1_bias, grad_fc2_bias = [
        packed[e - n : e] for e, n in zip(ends, sizes)
    ]
    act_all = jax.nn.silu(cond_all.astype(f32)).astype(bf16)
    d_act_part = jnp.einsum("ic,dc->id", dmod_all, ada_weight, preferred_element_type=f32)
    d_act_cols = lax.psum_scatter(d_act_part, "tensor", scatter_dimension=1, tiled=True)
    silu_value, silu_pull = jax.vjp(jax.nn.silu, cond_all_cols)
    d_cond = silu_pull(d_act_cols)[0]
    grad_table = jnp.einsum(
        "in,ic->nc", pick_all.astype(f32), d_cond, precision=highest, preferred_element_type=f32
    )
    grad_ada = jnp.einsum("id,ic->dc", act_all, dmod_all, preferred_element_type=f32)
    grad_ada_bias = jnp.sum(dmod_all.astype(f32), axis=0)
    grad_qkv, grad_proj, grad_fc1, grad_fc2 = (
        lax.psum(grad_qkv.astype(bf16), "dp").astype(f32),
        lax.psum(grad_proj.astype(bf16), "dp").astype(f32),
        lax.psum(grad_fc1.astype(bf16), "dp").astype(f32),
        lax.psum(grad_fc2.astype(bf16), "dp").astype(f32),
    )
    return (
        result,
        d_tokens,
        grad_table,
        grad_ada,
        grad_ada_bias,
        grad_qkv,
        grad_q_bias,
        grad_v_bias,
        grad_scale,
        grad_proj,
        grad_proj_bias,
        grad_fc1,
        grad_fc1_bias,
        grad_fc2,
        grad_fc2_bias,
    )


def solution(mesh):
    return jax.shard_map(
        per_device,
        mesh=mesh,
        in_specs=(
            P("dp", None),
            P("dp", None),
            P(),
            P("dp", None),
            P(None, "tensor"),
            P(None, "tensor"),
            P("tensor"),
            P(None, None, "tensor"),
            P("tensor"),
            P("tensor"),
            P("tensor"),
            P("tensor", None),
            P(),
            P(None, "tensor"),
            P("tensor"),
            P("tensor", None),
            P(),
        ),
        out_specs=(
            P("dp", None),
            P("dp", None),
            P(None, "tensor"),
            P(None, "tensor"),
            P("tensor"),
            P(None, None, "tensor"),
            P("tensor"),
            P("tensor"),
            P("tensor"),
            P("tensor", None),
            P(),
            P(None, "tensor"),
            P("tensor"),
            P("tensor", None),
            P(),
        ),
        check_vma=False,
    )
```

profile of v0, /device:TPU:0, one launch (start us, length us, event | category | flops | bytes accessed | tf_op | source)
XLA Modules:
  0.0 914.1 jit_solution(17370807732758407328)
XLA Ops:
  33.7 6.9 convolution_add_fusion
  40.6 12.9 %reshape.303 = f32[2,680,3,8,64]{4,3,1,0,2:T(8,128)} reshape(f32[1360,3,512]{2,0,1:T(8,128)} %convolution_add_fusion) | data formatting | bytes 16711680 | tf_op jit(solution)/shard_map/reshape | solution.py:82
  58.0 9.3 %fusion.104 = (f32[2,680,1,8,64]{4,3,1,0,2:T(8,128)}, f32[2,680,1,8,64]{4,3,1,0,2:T(8,128)}) fusion(f32[2,680,3,8,64]{4,3,1,0,2:T(8,128)} %reshape.303), kind=kLoop, calls=%fused_computation.175 | loop fusion | bytes 11141120 | tf_op jit(solution)/shard_map/slice | solution.py:83
  81.4 6.0 copy.107
  89.7 16.8 %select_reduce_fusion = (f32[2,8,680]{2,1,0:T(8,128)S(1)}, f32[2,8,680,680]{2,3,1,0:T(8,128)}) fusion(pred[2,680,680]{1,2,0:T(8,128)(4,1)} %broadcast_compare_fusion, f32[2,680,1,8,64]{1,4,3,0,2:T(8,128)} %copy.107, f32[2,680,8]{1,2,0:T(8,128)S(1)} %get-tuple-element.67, f32[2,680,1,8,64]{1,4,3,0,2:T(8,128)} %copy.106, f32[8]{0:T(128)S(1)} %exp.22, ...), kind=kOutput, calls=%fused_computation.8 | convolution fusion | flops 965262720 | bytes 36219552 | tf_op jit(solution)/shard_map/ishe,ithe->ihst/dot_general | solution.py:98
  106.5 14.0 %fusion.2 = f32[2,8,680]{2,1,0:T(8,128)S(1)} fusion(f32[2,8,680,680]{2,3,1,0:T(8,128)} %get-tuple-element.62, f32[2,8,680]{2,1,0:T(8,128)S(1)} %get-tuple-element.61, pred[2,680,680]{1,2,0:T(8,128)(4,1)S(1)} %copy-done.8), kind=kLoop, calls=%fused_computation.7 | loop fusion | flops 22184320 | bytes 30605440 | tf_op jit(solution)/shard_map/reduce_sum | solution.py:104
  120.5 16.6 %fusion.51 = bf16[2,680,8,64]{1,3,2,0:T(8,128)(2,1)} fusion(f32[2,8,680,680]{2,3,1,0:T(8,128)} %get-tuple-element.62, f32[2,8,680]{2,1,0:T(8,128)S(1)} %fusion.2, f32[2,8,680]{2,1,0:T(8,128)S(1)} %get-tuple-element.61, pred[2,680,680]{1,2,0:T(8,128)(4,1)S(1)} %copy-done.8, bf16[2,680,1,8,64]{1,4,3,0,2:T(8,128)(2,1)} %copy.105), kind=kOutput, calls=%fused_computation.104 | convolution fusion | flops 977285120 | bytes 33390720 | tf_op jit(solution)/shard_map/ihst,ithe->ishe/dot_general | solution.py:108
  159.3 52.3 %collective-permute-done = bf16[1360,1024]{1,0:T(8,128)(2,1)} collective-permute-done((bf16[1360,1024]{1,0:T(8,128)(2,1)}, bf16[1360,1024]{1,0:T(8,128)(2,1)}, u32[]{:S(2)}, u32[]{:S(2)}) %collective-permute-start) | collective-permute-done | bytes 2785312 | tf_op jit(solution)/shard_map/ppermute | solution.py:13
  211.6 6.6 bitcast_multiply_fusion.3
  222.9 8.7 fusion.108
  231.7 11.3 %convolution_convert_fusion.1 = bf16[1360,1024]{1,0:T(8,128)(2,1)} fusion(bf16[2048,1024]{1,0:T(8,128)(2,1)S(1)} %copy-done.45, f32[1360,2048]{1,0:T(8,128)} %fusion.108, f32[2048]{0:T(1024)S(1)} %convert_element_type.198), kind=kOutput, calls=%fused_computation.63 | convolution fusion | flops 5733498880 | bytes 18128896 | tf_op jit(solution)/shard_map/dot_general | solution.py:123
  244.8 16.8 %convert_reduce_fusion = (f32[2048]{0:T(1024)}, bf16[1360,2048]{1,0:T(8,128)(2,1)}) fusion(f32[1360,2048]{1,0:T(8,128)} %fusion.108, f32[2048]{0:T(1024)S(1)} %convert_element_type.198, bf16[1360,1024]{1,0:T(8,128)(2,1)S(1)} %get-tuple-element.30, bf16[2048,1024]{1,0:T(8,128)(2,1)S(1)} %copy-done.45), kind=kOutput, calls=%fused_computation.24 | convolution fusion | flops 5768312832 | bytes 23707648 | tf_op jit(solution)/shard_map/rd,fd->rf/dot_general | solution.py:129
  261.6 10.0 %convolution_convert_fusion = bf16[1360,1024]{1,0:T(8,128)(2,1)} fusion(bf16[1360,2048]{1,0:T(8,128)(2,1)} %get-tuple-element.32, bf16[1024,2048]{1,0:T(8,128)(2,1)S(1)} %copy-done.46), kind=kOutput, calls=%fused_computation.62 | convolution fusion | flops 5705646080 | bytes 12550144 | tf_op jit(solution)/shard_map/rf,df->rd/dot_general | solution.py:135
  271.9 12.8 %convolution_convert_fusion.2 = bf16[2048,1024]{1,0:T(8,128)(2,1)} fusion(bf16[1360,1024]{1,0:T(8,128)(2,1)S(1)} %get-tuple-element.30, f32[1360,2048]{1,0:T(8,128)} %fusion.108, f32[2048]{0:T(1024)S(1)} %convert_element_type.198), kind=kOutput, calls=%fused_computation.64 | convolution fusion | flops 5734203392 | bytes 18128896 | tf_op jit(solution)/shard_map/rf,rd->fd/dot_general | solution.py:127
  284.9 77.4 %collective-permute-done.2 = bf16[1360,1024]{1,0:T(8,128)(2,1)} collective-permute-done((bf16[1360,1024]{1,0:T(8,128)(2,1)}, bf16[1360,1024]{1,0:T(8,128)(2,1)}, u32[]{:S(2)}, u32[]{:S(2)}) %collective-permute-start.2) | collective-permute-done | bytes 2785312 | tf_op jit(solution)/shard_map/ppermute | solution.py:13
  365.5 7.7 fusion.99
  373.3 12.9 %convert_reduce_fusion.2 = (f32[1024]{0:T(1024)S(1)}, bf16[1360,1024]{1,0:T(8,128)(2,1)}, f32[1360,1024]{1,0:T(8,128)}, f32[1360,1024]{1,0:T(8,128)}, bf16[1360,1024]{1,0:T(8,128)(2,1)}, /*index=5*/f32[1360,1024]{1,0:T(8,128)}) fusion(f32[2,1024]{1,0:T(2,128)S(1)} %get-tuple-element.54, f32[1360]{0:T(1024)S(1)} %broadcast_multiply_fusion.2, ...), kind=kLoop, calls=%fused_computation.40 | loop fusion | flops 32029696 | bytes 41833728 | tf_op jit(solution)/shard_map/reduce_sum | solution.py:141
  399.4 16.6 %fusion.48 = bf16[2,680,8,64]{1,3,2,0:T(8,128)(2,1)} fusion(bf16[2,680,8,64]{1,3,2,0:T(8,128)(2,1)} %copy.84, f32[2,8,680,680]{2,3,1,0:T(8,128)} %get-tuple-element.62, f32[2,8,680]{2,1,0:T(8,128)S(1)} %log_add_fusion, pred[2,680,680]{1,2,0:T(8,128)(4,1)} %broadcast_compare_fusion), kind=kOutput, calls=%fused_computation.102 | convolution fusion | flops 969886720 | bytes 33347200 | tf_op jit(solution)/shard_map/ihst,ishe->ithe/dot_general | solution.py:154
  416.1 30.7 %multiply_reduce_fusion = (f32[2,8,680]{2,1,0:T(8,128)S(1)}, f32[2,8,680,680]{2,3,1,0:T(8,128)}) fusion(f32[2,8,680,680]{2,3,1,0:T(8,128)} %get-tuple-element.62, f32[2,8,680]{2,1,0:T(8,128)S(1)} %log_add_fusion, pred[2,680,680]{1,2,0:T(8,128)(4,1)} %broadcast_compare_fusion, bf16[2,680,8,64]{1,3,2,0:T(8,128)(2,1)} %copy.84, ...), kind=kOutput, calls=%fused_computation.3 | convolution fusion | flops 976577920 | bytes 62984320 | tf_op jit(solution)/shard_map/ishe,ithe->ihst/dot_general | solution.py:148
  446.8 28.4 %multiply_convert_fusion = bf16[2,8,680,680]{2,3,1,0:T(8,128)(2,1)} fusion(f32[2,8,680,680]{2,3,1,0:T(8,128)} %get-tuple-element.64, f32[2,8,680,680]{2,3,1,0:T(8,128)} %get-tuple-element.62, f32[2,8,680]{2,1,0:T(8,128)S(1)} %get-tuple-element.63, f32[2,8,680]{2,1,0:T(8,128)S(1)} %log_add_fusion, pred[2,680,680]{1,2,0:T(8,128)(4,1)} %broadcast_compare_fusion), kind=kLoop, calls=%fused_computation.2 | loop fusion | flops 36992000 | bytes 74995840 | tf_op jit(solution)/shard_map/convert_element_type | solution.py:151
  475.2 11.5 %fusion.97 = f32[2,8,64,680]{3,2,1,0:T(8,128)} fusion(bf16[2,8,680,680]{2,3,1,0:T(8,128)(2,1)} %multiply_convert_fusion, f32[2,680,1,8,64]{1,4,3,0,2:T(8,128)} %copy.106, f32[8]{0:T(128)S(1)} %copy-done.31, f32[2,680,8]{1,2,0:T(8,128)S(1)} %copy-done.12), kind=kOutput, calls=%fused_computation.171 | convolution fusion | flops 949084160 | bytes 20410912 | tf_op jit(solution)/shard_map/ihst,ishe->ithe/dot_general | solution.py:153
  486.7 10.5 %fusion.25 = (f32[8]{0:T(128)S(1)}, f32[2,8,64,680]{3,2,1,0:T(8,128)}) fusion(f32[2,680,1,8,64]{1,4,3,0,2:T(8,128)S(1)} %copy-done.5, f32[8]{0:T(128)S(1)} %copy-done.31, f32[2,680,8]{1,2,0:T(8,128)S(1)} %copy-done.12, bf16[2,8,680,680]{2,3,1,0:T(8,128)(2,1)} %multiply_convert_fusion, f32[2,680,1,8,64]{1,4,3,0,2:T(8,128)S(1)} %copy-done.7, ...), kind=kOutput, calls=%fused_computation.74 | convolution fusion | flops 951173120 | bytes 23239744 | tf_op jit(solution)/shard_map/ihst,ithe->ishe/dot_general | solution.py:152
  507.2 6.8 fusion.24
  534.1 8.2 bitcast_convert_fusion
  543.7 11.0 %convolution_convert_fusion.3 = bf16[1024,2048]{1,0:T(8,128)(2,1)} fusion(bf16[1360,1024]{1,0:T(8,128)(2,1)S(1)} %copy-done.17, bf16[1360,2048]{1,0:T(8,128)(2,1)} %get-tuple-element.32), kind=kOutput, calls=%fused_computation.65 | convolution fusion | flops 5706350592 | bytes 12550144 | tf_op jit(solution)/shard_map/rd,rf->df/dot_general | solution.py:132
  559.6 9.5 %fusion.35 = bf16[1024,3,512]{2,0,1:T(8,128)(2,1)} fusion(bf16[1360,1024]{1,0:T(8,128)(2,1)} %copy-done.15, bf16[1360,1,512]{2,0,1:T(8,128)(2,1)} %copy.94, bf16[1360,1,512]{2,0,1:T(8,128)(2,1)} %reshape.302, bf16[1360,1,512]{2,0,1:T(8,128)(2,1)} %copy.92), kind=kOutput, calls=%fused_computation.92 | convolution fusion | flops 4292296704 | bytes 10108928 | tf_op jit(solution)/shard_map/rd,rpc->dpc/dot_general | solution.py:168
  569.1 31.9 %collective-permute-done.3 = bf16[1360,1024]{1,0:T(8,128)(2,1)} collective-permute-done((bf16[1360,1024]{1,0:T(8,128)(2,1)}, bf16[1360,1024]{1,0:T(8,128)(2,1)}, u32[]{:S(2)}, u32[]{:S(2)}) %collective-permute-start.3) | collective-permute-done | bytes 2785312 | tf_op jit(solution)/shard_map/ppermute | solution.py:13
  604.2 6.5 fusion.98
  616.3 9.5 %multiply_reduce_fusion.1 = (bf16[2,1024]{1,0:T(2,128)(2,1)S(1)}, bf16[2,1024]{1,0:T(2,128)(2,1)S(1)}, bf16[2,1024]{1,0:T(2,128)(2,1)S(1)}, bf16[2,1024]{1,0:T(2...) fusion(f32[2,680,1024]{2,1,0:T(8,128)} %bitcast.179, f32[2,680,1024]{2,1,0:T(8,128)S(1)} %bitcast.178, ...), kind=kLoop, calls=%fused_computation.41 | loop fusion | flops 33411072 | bytes 27926400 | tf_op jit(solution)/shard_map/reduce_sum | solution.py:180
  625.9 21.9 %all-gather.1 = bf16[16,2,3072]{2,1,0:T(2,128)(2,1)S(1)} all-gather(bf16[1,2,3072]{2,1,0:T(2,128)(2,1)S(1)} %dynamic-slice_bitcast_fusion), channel_id=1, replica_groups=mesh['dp'=16,'tensor'=2] {'dp'}, dimensions={0}, use_global_device_ids=true | all-gather | bytes 208896 | tf_op jit(solution)/shard_map/all_gather | solution.py:188
  664.8 6.6 fusion.66
  674.6 214.2 %all-reduce.7.cloned.1.call-done = (bf16[1024,3,512]{2,0,1:T(8,128)(2,1)}, bf16[512,1024]{1,0:T(8,128)(2,1)}, bf16[1024,2048]{1,0:T(8,128)(2,1)}, bf16[2048,1024]{1,0:T(8,128)(2,1)}) async-done(((bf16[1024,3,512]{2,0,1:T(8,128)(2,1)}, bf16[512,1024]{1,0:T(8,128)(2,1)}, bf16[1024,2048]{1,0:T(8,128)(2,1)}, bf16[2048,1024]{1,0:T(8,128)(2,1)}), (bf16[1024,3,512]{2,0,1:T(8,128)(2,1)}, ...) | async-done | bytes 12582928 | tf_op jit(solution)/shard_map/psum | solution.py:208
  (217 shorter events, 174.1 us)
Async XLA Ops:
  8.0 25.7 %copy-start = (bf16[1024,3,512]{2,0,1:T(8,128)(2,1)S(1)}, bf16[1024,3,512]{2,0,1:T(8,128)(2,1)}, u32[]{:S(2)}) copy-start(bf16[1024,3,512]{2,0,1:T(8,128)(2,1)} %param.24) | copy-start | bytes 9437188
  8.1 650.7 %all-reduce.5.cloned.1.call-start = ((), (), s32[]{:S(2)}) async-start(), calls=%async_computation.2 | async-start | bytes 663552
  12.0 141.3 %copy-start.25 = (f32[1360]{0:T(1024)}, f32[1360]{0:T(1024)S(1)}, u32[]{:S(2)}) copy-start(f32[1360]{0:T(1024)S(1)} %broadcast_multiply_fusion.5) | copy-start | bytes 16324
  14.7 139.2 %copy-start.28 = (f32[1360]{0:T(1024)}, f32[1360]{0:T(1024)S(1)}, u32[]{:S(2)}) copy-start(f32[1360]{0:T(1024)S(1)} %add_rsqrt_fusion.3) | copy-start | bytes 16324
  21.2 11.1 %copy-start.23 = (bf16[32,1024]{1,0:T(8,128)(2,1)}, bf16[32,1024]{1,0:T(8,128)(2,1)S(1)}, u32[]{:S(2)}) copy-start(bf16[32,1024]{1,0:T(8,128)(2,1)S(1)} %all_gather.15) | copy-start | bytes 196612
  29.5 11.1 %copy-start.32 = (f32[2,1024]{1,0:T(2,128)}, f32[2,1024]{1,0:T(2,128)S(1)}, u32[]{:S(2)}) copy-start(f32[2,1024]{1,0:T(2,128)S(1)} %get-tuple-element.53) | copy-start | bytes 24580
  67.3 22.4 %copy-start.30 = (f32[8]{0:T(128)}, f32[8]{0:T(128)S(1)}, u32[]{:S(2)}) copy-start(f32[8]{0:T(128)S(1)} %exp.22) | copy-start | bytes 100
  89.6 16.8 %copy-start.11 = (f32[2,680,8]{1,2,0:T(8,128)}, f32[2,680,8]{1,2,0:T(8,128)S(1)}, u32[]{:S(2)}) copy-start(f32[2,680,8]{1,2,0:T(8,128)S(1)} %get-tuple-element.68) | copy-start | bytes 130564
  89.6 16.8 %copy-start.18 = (f32[2,680,8]{1,2,0:T(8,128)}, f32[2,680,8]{1,2,0:T(8,128)S(1)}, u32[]{:S(2)}) copy-start(f32[2,680,8]{1,2,0:T(8,128)S(1)} %get-tuple-element.67) | copy-start | bytes 130564
  89.7 16.8 %copy-start.8 = (pred[2,680,680]{1,2,0:T(8,128)(4,1)S(1)}, pred[2,680,680]{1,2,0:T(8,128)(4,1)}, u32[]{:S(2)}) copy-start(pred[2,680,680]{1,2,0:T(8,128)(4,1)} %broadcast_compare_fusion) | copy-start | bytes 2774404
  151.2 60.4 %collective-permute-start = (bf16[1360,1024]{1,0:T(8,128)(2,1)}, bf16[1360,1024]{1,0:T(8,128)(2,1)}, u32[]{:S(2)}, u32[]{:S(2)}) collective-permute-start(bf16[1360,1024]{1,0:T(8,128)(2,1)} %convolution_convert_fusion.4), channel_id=1, source_target_pairs={{0,1},{1,0},{2,3},{3,2},{4,5},{5,4},{6,7},{7,6},{8,9},{9,8},{10,11... | collective-permute-start | bytes 8355848 | tf_op jit(solution)/shard_map/ppermute | solution.py:13
  243.0 130.2 %collective-permute-start.1 = (bf16[1360,1024]{1,0:T(8,128)(2,1)}, bf16[1360,1024]{1,0:T(8,128)(2,1)}, u32[]{:S(2)}, u32[]{:S(2)}) collective-permute-start(bf16[1360,1024]{1,0:T(8,128)(2,1)} %convolution_convert_fusion.1), channel_id=1, source_target_pairs={{0,1},{1,0},{2,3},{3,2},{4,5},{5,4},{6,7},{7,6},{8,9},{9,8},{10,11... | collective-permute-start | bytes 8355848 | tf_op jit(solution)/shard_map/ppermute | solution.py:13
  271.6 90.7 %collective-permute-start.2 = (bf16[1360,1024]{1,0:T(8,128)(2,1)}, bf16[1360,1024]{1,0:T(8,128)(2,1)}, u32[]{:S(2)}, u32[]{:S(2)}) collective-permute-start(bf16[1360,1024]{1,0:T(8,128)(2,1)} %convolution_convert_fusion), channel_id=1, source_target_pairs={{0,1},{1,0},{2,3},{3,2},{4,5},{5,4},{6,7},{7,6},{8,9},{9,8},{10,11... | collective-permute-start | bytes 8355848 | tf_op jit(solution)/shard_map/ppermute | solution.py:13
  362.3 11.0 %slice-start = ((s8[5570560]{0:T(1024)(128)(4,1)}), s8[4194304]{0:T(1024)(128)(4,1)S(1)}, s32[]{:S(2)}) async-start(s8[5570560]{0:T(1024)(128)(4,1)} %bitcast.169), calls=%async_computation.4 | async-start | bytes 8388608
  373.2 12.9 %copy-start.47 = (bf16[512,1024]{1,0:T(8,128)(2,1)S(1)}, bf16[512,1024]{1,0:T(8,128)(2,1)}, u32[]{:S(2)}) copy-start(bf16[512,1024]{1,0:T(8,128)(2,1)} %param.28) | copy-start | bytes 3145732
  446.8 28.4 %copy-start.12 = (f32[2,680,8]{1,2,0:T(8,128)S(1)}, f32[2,680,8]{1,2,0:T(8,128)}, u32[]{:S(2)}) copy-start(f32[2,680,8]{1,2,0:T(8,128)} %copy-done.11) | copy-start | bytes 130564
  446.8 28.4 %copy-start.31 = (f32[8]{0:T(128)S(1)}, f32[8]{0:T(128)}, u32[]{:S(2)}) copy-start(f32[8]{0:T(128)} %copy-done.30) | copy-start | bytes 100
  475.2 11.5 %copy-start.5 = (f32[2,680,1,8,64]{1,4,3,0,2:T(8,128)S(1)}, f32[2,680,1,8,64]{1,4,3,0,2:T(8,128)}, u32[]{:S(2)}) copy-start(f32[2,680,1,8,64]{1,4,3,0,2:T(8,128)} %copy.106) | copy-start | bytes 8355844
  475.2 11.5 %copy-start.7 = (f32[2,680,1,8,64]{1,4,3,0,2:T(8,128)S(1)}, f32[2,680,1,8,64]{1,4,3,0,2:T(8,128)}, u32[]{:S(2)}) copy-start(f32[2,680,1,8,64]{1,4,3,0,2:T(8,128)} %copy.107) | copy-start | bytes 8355844
  475.2 11.5 %copy-start.19 = (f32[2,680,8]{1,2,0:T(8,128)S(1)}, f32[2,680,8]{1,2,0:T(8,128)}, u32[]{:S(2)}) copy-start(f32[2,680,8]{1,2,0:T(8,128)} %copy-done.18) | copy-start | bytes 130564
  486.7 10.5 %copy-start.20 = (bf16[2,680,8,64]{1,3,2,0:T(8,128)(2,1)S(1)}, bf16[2,680,8,64]{1,3,2,0:T(8,128)(2,1)}, u32[]{:S(2)}) copy-start(bf16[2,680,8,64]{1,3,2,0:T(8,128)(2,1)} %fusion.48) | copy-start | bytes 4177924
  542.3 15.9 %copy-start.37 = (f32[1024]{0:T(1024)S(1)}, f32[1024]{0:T(1024)}, u32[]{:S(2)}) copy-start(f32[1024]{0:T(1024)} %get-tuple-element.29) | copy-start | bytes 12292
  542.3 15.9 %copy-start.38 = (f32[2048]{0:T(1024)S(1)}, f32[2048]{0:T(1024)}, u32[]{:S(2)}) copy-start(f32[2048]{0:T(1024)} %get-tuple-element.31) | copy-start | bytes 24580
  542.3 58.7 %collective-permute-start.3 = (bf16[1360,1024]{1,0:T(8,128)(2,1)}, bf16[1360,1024]{1,0:T(8,128)(2,1)}, u32[]{:S(2)}, u32[]{:S(2)}) collective-permute-start(bf16[1360,1024]{1,0:T(8,128)(2,1)} %bitcast_convert_fusion), channel_id=1, source_target_pairs={{0,1},{1,0},{2,3},{3,2},{4,5},{5,4},{6,7},{7,6},{8,9},{9,8},{10,11... | collective-permute-start | bytes 8355848 | tf_op jit(solution)/shard_map/ppermute | solution.py:13
  559.5 41.4 %copy-start.33 = (f32[2,1024]{1,0:T(2,128)S(1)}, f32[2,1024]{1,0:T(2,128)}, u32[]{:S(2)}) copy-start(f32[2,1024]{1,0:T(2,128)} %copy-done.32) | copy-start | bytes 24580
  559.5 111.9 %reduce-scatter.2.cloned.1.call-start = ((), (), s32[]{:S(2)}) async-start(), calls=%async_computation.1 | async-start | bytes 196608 | tf_op jit(solution)/shard_map/reduce_scatter | solution.py:199
  569.1 35.1 %copy-start.4 = (bf16[1360,1024]{1,0:T(8,128)(2,1)S(1)}, bf16[1360,1024]{1,0:T(8,128)(2,1)}, u32[]{:S(2)}) copy-start(bf16[1360,1024]{1,0:T(8,128)(2,1)} %param.17) | copy-start | bytes 8355844
  569.1 35.1 %copy-start.26 = (f32[1360]{0:T(1024)S(1)}, f32[1360]{0:T(1024)}, u32[]{:S(2)}) copy-start(f32[1360]{0:T(1024)} %copy-done.25) | copy-start | bytes 16324
  569.1 35.1 %copy-start.29 = (f32[1360]{0:T(1024)S(1)}, f32[1360]{0:T(1024)}, u32[]{:S(2)}) copy-start(f32[1360]{0:T(1024)} %copy-done.28) | copy-start | bytes 16324
  600.9 9.8 %slice-start.2 = ((s8[5570560]{0:T(1024)(128)(4,1)}), s8[4194304]{0:T(1024)(128)(4,1)S(1)}, s32[]{:S(2)}) async-start(s8[5570560]{0:T(1024)(128)(4,1)} %bitcast.174), calls=%async_computation.6 | async-start | bytes 8388608
  604.2 12.1 %slice-start.4 = ((s8[5570560]{0:T(1024)(128)(4,1)}), s8[4194304]{0:T(1024)(128)(4,1)S(1)}, s32[]{:S(2)}) async-start(s8[5570560]{0:T(1024)(128)(4,1)} %bitcast.176), calls=%async_computation.8 | async-start | bytes 8388608
  653.3 235.5 %all-reduce.7.cloned.1.call-start = ((), (), s32[]{:S(2)}) async-start(), calls=%async_computation.3 | async-start | bytes 25165824 | tf_op jit(solution)/shard_map/psum | solution.py:208
  (31 other events, 204.8 us)
Sparse Core Ops, SparseCore 0:
  559.6 89.7 all-reduce.4
  659.3 229.5 all-reduce.6
Sparse Core Ops, SparseCore 1:
  653.4 7.6 reduce-scatter.1
where the time goes:
time: 920 us; the launch traced here: 914 us
  waiting for transfers between devices  376 us (41%)
  matrix products  232 us (25%)
  other arithmetic  144 us (16%)
  local copies, waits for them, and re-layouts  107 us (12%)
  blocking collectives  31.9 us (3%)
  between operations  17.4 us (2%)
    psum x1, waiting for transfers between devices, per_device(): lax.psum(grad_qkv.astype(bf16), 'dp').astype(f32)  214 us
    ppermute x4, waiting for transfers between devices, tensor_sum(): other = lax.ppermute(part, 'tensor', [(0, 1), (1, 0)])  162 us
    dot_general x1, matrix products, per_device(): jnp.einsum('ishe,ithe->ihst', d_attn, value_low, preferred_element_type=f32)  30.7 us
    convert_element_type x1, other arithmetic, per_device(): d_scores = (again_probs * (d_probs - jnp.sum(again_probs * d_probs, axis=...  28.4 us
    another operation x6, local copies, waits for them, and re-layouts, per_device(): jnp.stack([d_query, d_key, d_value], axis=2)  23.5 us
    all_gather x1, blocking collectives, per_device(): dmod_all = lax.all_gather(dmod_cols, 'dp', axis=0, tiled=True)  21.9 us
    unnamed x125, local copies, waits for them, and re-layouts  20.8 us
  transfers between devices with their start and end apart: 7, of which 4 were waited for; matrix products, arithmetic and copies ran while one was open for 14% of the time, Pallas kernels for 0%

commit v1 on v0

--- a/solution.py
+++ b/solution.py
@@ -6,6 +6,22 @@
 
 epsilon = 1e-06
 highest = lax.Precision.HIGHEST
+
+
+def ring_gather(x, axis, dim):
+    ways, here, hop = (lax.axis_size(axis), lax.axis_index(axis), x.shape[dim])
+    dims = [n * ways if d == dim else n for d, n in enumerate(x.shape)]
+    full = lax.dynamic_update_slice_in_dim(jnp.zeros(dims, x.dtype), x, here * hop, axis=dim)
+    going_up = going_down = x
+    for far in range(1, ways // 2 + 1):
+        going_up = lax.ppermute(going_up, axis, [(d, (d + 1) % ways) for d in range(ways)])
+        full = lax.dynamic_update_slice_in_dim(full, going_up, (here - far) % ways * hop, axis=dim)
+        if 2 * far < ways:
+            going_down = lax.ppermute(going_down, axis, [(d, (d - 1) % ways) for d in range(ways)])
+            full = lax.dynamic_update_slice_in_dim(
+                full, going_down, (here + far) % ways * hop, axis=dim
+            )
+    return full
 
 
 def tensor_sum(part):
@@ -185,7 +201,7 @@
     ).astype(bf16)
     col_start = lax.axis_index("tensor") * mod_width
     dmod_cols = lax.dynamic_slice_in_dim(d_modul, col_start, mod_width, 1)
-    dmod_all = lax.all_gather(dmod_cols, "dp", axis=0, tiled=True)
+    dmod_all = ring_gather(dmod_cols, "dp", 0)
     small = [grad_q_bias, grad_v_bias, grad_scale, grad_proj_bias, grad_fc1_bias, grad_fc2_bias]
     sizes = [item.shape[0] for item in small]
     packed = lax.all_gather(jnp.concatenate(small), "dp", axis=0, tiled=False)

time: 920 us -> 991 us (1.077)
  waiting for transfers between devices: 376 us -> 437 us
  starting transfers between devices: 5.94 us -> 37.1 us
  blocking collectives: 31.9 us -> 9.99 us
    unnamed x4, waiting for transfers between devices: 0.07 us -> 36.3 us
    ppermute x0 -> x15, starting transfers between devices: none -> 31.2 us  [the longest x7 31.1 us: ring_gather(): lax.ppermute(going_down, axis, [(d, (d - 1) % ways) for d in range(ways)])]
    all_gather x1 -> x0, blocking collectives: 21.9 us -> none  [per_device(): dmod_all = lax.all_gather(dmod_cols, 'dp', axis=0, tiled=True)]
    ppermute x0 -> x15, waiting for transfers between devices: none -> 13.7 us  [the longest x8 13.4 us: ring_gather(): lax.ppermute(going_up, axis, [(d, (d + 1) % ways) for d in range(ways)])]
    unnamed x125 -> x123, local copies, waits for them, and re-layouts: 20.8 us -> 21.7 us
  transfers between devices with their start and end apart: 7 -> 22, of which waited for: 4 -> 16; matrix products, arithmetic and copies ran while one was open for 14% -> 11% of each run, Pallas kernels for 0% -> 0%
where the time goes in v1:
time: 991 us; the launch traced here: 985 us
  waiting for transfers between devices  437 us (44%)
  matrix products  233 us (24%)
  other arithmetic  142 us (14%)
  local copies, waits for them, and re-layouts  108 us (11%)
  starting transfers between devices  37.1 us (4%)
  between operations  17.3 us (2%)
  blocking collectives  9.99 us (1%)
    psum x1, waiting for transfers between devices, per_device(): lax.psum(grad_qkv.astype(bf16), 'dp').astype(f32)  222 us
    ppermute x4, waiting for transfers between devices, tensor_sum(): other = lax.ppermute(part, 'tensor', [(0, 1), (1, 0)])  164 us
    unnamed x4, waiting for transfers between devices  36.3 us
    ppermute x7, starting transfers between devices, ring_gather(): lax.ppermute(going_down, axis, [(d, (d - 1) % ways) for d in range(ways)])  31.1 us
    dot_general x1, matrix products, per_device(): jnp.einsum('ishe,ithe->ihst', d_attn, value_low, preferred_element_type=f32)  30.9 us
    convert_element_type x1, other arithmetic, per_device(): d_scores = (again_probs * (d_probs - jnp.sum(again_probs * d_probs, axis=...  28.4 us
    another operation x6, local copies, waits for them, and re-layouts, per_device(): jnp.stack([d_query, d_key, d_value], axis=2)  23.7 us
    unnamed x123, local copies, waits for them, and re-layouts  21.7 us
  transfers between devices with their start and end apart: 22, of which 16 were waited for; matrix products, arithmetic and copies ran while one was open for 11% of the time, Pallas kernels for 0%

profile of v1, /device:TPU:0, one launch (start us, length us, event | category | flops | bytes accessed | tf_op | source)
XLA Modules:
  0.0 984.9 jit_solution(6672144057323604511)
XLA Ops:
  33.7 7.0 convolution_add_fusion
  40.7 12.8 %reshape.301 = f32[2,680,3,8,64]{4,3,1,0,2:T(8,128)} reshape(f32[1360,3,512]{2,0,1:T(8,128)} %convolution_add_fusion) | data formatting | bytes 16711680 | tf_op jit(solution)/shard_map/reshape | solution.py:98
  58.1 9.3 fusion.102
  81.4 5.9 copy.89
  89.6 16.9 %select_reduce_fusion = (f32[2,8,680]{2,1,0:T(8,128)S(1)}, f32[2,8,680,680]{2,3,1,0:T(8,128)}) fusion(pred[2,680,680]{1,2,0:T(8,128)(4,1)} %broadcast_compare_fusion, f32[2,680,1,8,64]{1,4,3,0,2:T(8,128)} %copy.89, f32[2,680,8]{1,2,0:T(8,128)S(1)} %get-tuple-element.69, f32[2,680,1,8,64]{1,4,3,0,2:T(8,128)} %copy.88, f32[8]{0:T(128)S(1)} %exp.22, ...), kind=kOutput, calls=%fused_computation.8 | convolution fusion | flops 965262720 | bytes 36219552 | tf_op jit(solution)/shard_map/ishe,ithe->ihst/dot_general | solution.py:114
  106.6 14.0 %fusion.2 = f32[2,8,680]{2,1,0:T(8,128)S(1)} fusion(f32[2,8,680,680]{2,3,1,0:T(8,128)} %get-tuple-element.64, f32[2,8,680]{2,1,0:T(8,128)S(1)} %get-tuple-element.63, pred[2,680,680]{1,2,0:T(8,128)(4,1)S(1)} %copy-done.8), kind=kLoop, calls=%fused_computation.7 | loop fusion | flops 22184320 | bytes 30605440 | tf_op jit(solution)/shard_map/reduce_sum | solution.py:120
  120.6 16.8 %fusion.51 = bf16[2,680,8,64]{1,3,2,0:T(8,128)(2,1)} fusion(f32[2,8,680,680]{2,3,1,0:T(8,128)} %get-tuple-element.64, f32[2,8,680]{2,1,0:T(8,128)S(1)} %fusion.2, f32[2,8,680]{2,1,0:T(8,128)S(1)} %get-tuple-element.63, pred[2,680,680]{1,2,0:T(8,128)(4,1)S(1)} %copy-done.8, bf16[2,680,1,8,64]{1,4,3,0,2:T(8,128)(2,1)} %copy.87), kind=kOutput, calls=%fused_computation.104 | convolution fusion | flops 977285120 | bytes 33390720 | tf_op jit(solution)/shard_map/ihst,ithe->ishe/dot_general | solution.py:124
  159.4 52.2 %collective-permute-done = bf16[1360,1024]{1,0:T(8,128)(2,1)} collective-permute-done((bf16[1360,1024]{1,0:T(8,128)(2,1)}, bf16[1360,1024]{1,0:T(8,128)(2,1)}, u32[]{:S(2)}, u32[]{:S(2)}) %collective-permute-start) | collective-permute-done | bytes 2785312 | tf_op jit(solution)/shard_map/ppermute | solution.py:29
  211.7 6.6 bitcast_multiply_fusion.3
  223.0 8.7 fusion.106
  231.8 11.4 %convolution_convert_fusion.1 = bf16[1360,1024]{1,0:T(8,128)(2,1)} fusion(bf16[2048,1024]{1,0:T(8,128)(2,1)S(1)} %copy-done.45, f32[1360,2048]{1,0:T(8,128)} %fusion.106, f32[2048]{0:T(1024)S(1)} %convert_element_type.198), kind=kOutput, calls=%fused_computation.63 | convolution fusion | flops 5733498880 | bytes 18128896 | tf_op jit(solution)/shard_map/dot_general | solution.py:139
  244.9 16.8 %convert_reduce_fusion = (f32[2048]{0:T(1024)}, bf16[1360,2048]{1,0:T(8,128)(2,1)}) fusion(f32[1360,2048]{1,0:T(8,128)} %fusion.106, f32[2048]{0:T(1024)S(1)} %convert_element_type.198, bf16[1360,1024]{1,0:T(8,128)(2,1)S(1)} %get-tuple-element.30, bf16[2048,1024]{1,0:T(8,128)(2,1)S(1)} %copy-done.45), kind=kOutput, calls=%fused_computation.24 | convolution fusion | flops 5768312832 | bytes 23707648 | tf_op jit(solution)/shard_map/rd,fd->rf/dot_general | solution.py:145
  261.7 10.0 %convolution_convert_fusion = bf16[1360,1024]{1,0:T(8,128)(2,1)} fusion(bf16[1360,2048]{1,0:T(8,128)(2,1)} %get-tuple-element.32, bf16[1024,2048]{1,0:T(8,128)(2,1)S(1)} %copy-done.46), kind=kOutput, calls=%fused_computation.62 | convolution fusion | flops 5705646080 | bytes 12550144 | tf_op jit(solution)/shard_map/rf,df->rd/dot_general | solution.py:151
  272.0 13.1 %convolution_convert_fusion.2 = bf16[2048,1024]{1,0:T(8,128)(2,1)} fusion(bf16[1360,1024]{1,0:T(8,128)(2,1)S(1)} %get-tuple-element.30, f32[1360,2048]{1,0:T(8,128)} %fusion.106, f32[2048]{0:T(1024)S(1)} %convert_element_type.198), kind=kOutput, calls=%fused_computation.64 | convolution fusion | flops 5734203392 | bytes 18128896 | tf_op jit(solution)/shard_map/rf,rd->fd/dot_general | solution.py:143
  285.2 77.2 %collective-permute-done.2 = bf16[1360,1024]{1,0:T(8,128)(2,1)} collective-permute-done((bf16[1360,1024]{1,0:T(8,128)(2,1)}, bf16[1360,1024]{1,0:T(8,128)(2,1)}, u32[]{:S(2)}, u32[]{:S(2)}) %collective-permute-start.2) | collective-permute-done | bytes 2785312 | tf_op jit(solution)/shard_map/ppermute | solution.py:29
  365.6 7.7 fusion.97
  373.4 12.9 %convert_reduce_fusion.2 = (f32[1024]{0:T(1024)S(1)}, bf16[1360,1024]{1,0:T(8,128)(2,1)}, f32[1360,1024]{1,0:T(8,128)}, f32[1360,1024]{1,0:T(8,128)}, bf16[1360,1024]{1,0:T(8,128)(2,1)}, /*index=5*/f32[1360,1024]{1,0:T(8,128)}) fusion(f32[2,1024]{1,0:T(2,128)S(1)} %get-tuple-element.56, f32[1360]{0:T(1024)S(1)} %broadcast_multiply_fusion.2, ...), kind=kLoop, calls=%fused_computation.40 | loop fusion | flops 32029696 | bytes 41833728 | tf_op jit(solution)/shard_map/reduce_sum | solution.py:157
  399.6 16.4 %fusion.48 = bf16[2,680,8,64]{1,3,2,0:T(8,128)(2,1)} fusion(bf16[2,680,8,64]{1,3,2,0:T(8,128)(2,1)} %copy.66, f32[2,8,680,680]{2,3,1,0:T(8,128)} %get-tuple-element.64, f32[2,8,680]{2,1,0:T(8,128)S(1)} %log_add_fusion, pred[2,680,680]{1,2,0:T(8,128)(4,1)} %broadcast_compare_fusion), kind=kOutput, calls=%fused_computation.102 | convolution fusion | flops 969886720 | bytes 33347200 | tf_op jit(solution)/shard_map/ihst,ishe->ithe/dot_general | solution.py:170
  416.0 30.9 %multiply_reduce_fusion = (f32[2,8,680]{2,1,0:T(8,128)S(1)}, f32[2,8,680,680]{2,3,1,0:T(8,128)}) fusion(f32[2,8,680,680]{2,3,1,0:T(8,128)} %get-tuple-element.64, f32[2,8,680]{2,1,0:T(8,128)S(1)} %log_add_fusion, pred[2,680,680]{1,2,0:T(8,128)(4,1)} %broadcast_compare_fusion, bf16[2,680,8,64]{1,3,2,0:T(8,128)(2,1)} %copy.66, ...), kind=kOutput, calls=%fused_computation.3 | convolution fusion | flops 976577920 | bytes 62984320 | tf_op jit(solution)/shard_map/ishe,ithe->ihst/dot_general | solution.py:164
  446.9 28.4 %multiply_convert_fusion = bf16[2,8,680,680]{2,3,1,0:T(8,128)(2,1)} fusion(f32[2,8,680,680]{2,3,1,0:T(8,128)} %get-tuple-element.66, f32[2,8,680,680]{2,3,1,0:T(8,128)} %get-tuple-element.64, f32[2,8,680]{2,1,0:T(8,128)S(1)} %get-tuple-element.65, f32[2,8,680]{2,1,0:T(8,128)S(1)} %log_add_fusion, pred[2,680,680]{1,2,0:T(8,128)(4,1)} %broadcast_compare_fusion), kind=kLoop, calls=%fused_computation.2 | loop fusion | flops 36992000 | bytes 74995840 | tf_op jit(solution)/shard_map/convert_element_type | solution.py:167
  475.4 11.5 %fusion.95 = f32[2,8,64,680]{3,2,1,0:T(8,128)} fusion(bf16[2,8,680,680]{2,3,1,0:T(8,128)(2,1)} %multiply_convert_fusion, f32[2,680,1,8,64]{1,4,3,0,2:T(8,128)} %copy.88, f32[8]{0:T(128)S(1)} %copy-done.31, f32[2,680,8]{1,2,0:T(8,128)S(1)} %copy-done.13), kind=kOutput, calls=%fused_computation.186 | convolution fusion | flops 949084160 | bytes 20410912 | tf_op jit(solution)/shard_map/ihst,ishe->ithe/dot_general | solution.py:169
  486.9 10.5 %fusion.25 = (f32[8]{0:T(128)S(1)}, f32[2,8,64,680]{3,2,1,0:T(8,128)}) fusion(f32[2,680,1,8,64]{1,4,3,0,2:T(8,128)S(1)} %copy-done.5, f32[8]{0:T(128)S(1)} %copy-done.31, f32[2,680,8]{1,2,0:T(8,128)S(1)} %copy-done.13, bf16[2,8,680,680]{2,3,1,0:T(8,128)(2,1)} %multiply_convert_fusion, f32[2,680,1,8,64]{1,4,3,0,2:T(8,128)S(1)} %copy-done.7, ...), kind=kOutput, calls=%fused_computation.74 | convolution fusion | flops 951173120 | bytes 23239744 | tf_op jit(solution)/shard_map/ihst,ithe->ishe/dot_general | solution.py:168
  507.3 6.8 fusion.24
  534.5 8.2 bitcast_convert_fusion
  544.1 11.0 %convolution_convert_fusion.3 = bf16[1024,2048]{1,0:T(8,128)(2,1)} fusion(bf16[1360,1024]{1,0:T(8,128)(2,1)S(1)} %copy-done.18, bf16[1360,2048]{1,0:T(8,128)(2,1)} %get-tuple-element.32), kind=kOutput, calls=%fused_computation.65 | convolution fusion | flops 5706350592 | bytes 12550144 | tf_op jit(solution)/shard_map/rd,rf->df/dot_general | solution.py:148
  556.9 9.4 fusion.35
  566.4 34.9 %collective-permute-done.3 = bf16[1360,1024]{1,0:T(8,128)(2,1)} collective-permute-done((bf16[1360,1024]{1,0:T(8,128)(2,1)}, bf16[1360,1024]{1,0:T(8,128)(2,1)}, u32[]{:S(2)}, u32[]{:S(2)}) %collective-permute-start.3) | collective-permute-done | bytes 2785312 | tf_op jit(solution)/shard_map/ppermute | solution.py:29
  604.6 6.5 fusion.96
  616.7 9.6 multiply_reduce_fusion.1
  685.2 36.2 %all-reduce.5.cloned.1.call-done = f32[82048]{0:T(1024)} async-done(((f32[82048]{0:T(1024)}), f32[82048]{0:T(1024)}) %all-reduce.5.cloned.1.call-update) | async-done | bytes 328208
  727.5 6.8 fusion.66
  737.5 222.4 %all-reduce.7.cloned.1.call-done = (bf16[1024,3,512]{2,0,1:T(8,128)(2,1)}, bf16[512,1024]{1,0:T(8,128)(2,1)}, bf16[1024,2048]{1,0:T(8,128)(2,1)}, bf16[2048,1024]{1,0:T(8,128)(2,1)}) async-done(((bf16[1024,3,512]{2,0,1:T(8,128)(2,1)}, bf16[512,1024]{1,0:T(8,128)(2,1)}, bf16[1024,2048]{1,0:T(8,128)(2,1)}, bf16[2048,1024]{1,0:T(8,128)(2,1)}), (bf16[1024,3,512]{2,0,1:T(8,128)(2,1)}, ...) | async-done | bytes 12582928 | tf_op jit(solution)/shard_map/psum | solution.py:224
  (261 shorter events, 218.8 us)
Async XLA Ops:
  8.0 25.7 %copy-start = (bf16[1024,3,512]{2,0,1:T(8,128)(2,1)S(1)}, bf16[1024,3,512]{2,0,1:T(8,128)(2,1)}, u32[]{:S(2)}) copy-start(bf16[1024,3,512]{2,0,1:T(8,128)(2,1)} %param.24) | copy-start | bytes 9437188
  8.1 713.4 %all-reduce.5.cloned.1.call-start = ((), (), s32[]{:S(2)}) async-start(), calls=%async_computation.2 | async-start | bytes 663552
  12.0 141.3 %copy-start.25 = (f32[1360]{0:T(1024)}, f32[1360]{0:T(1024)S(1)}, u32[]{:S(2)}) copy-start(f32[1360]{0:T(1024)S(1)} %broadcast_multiply_fusion.5) | copy-start | bytes 16324
  14.7 139.3 %copy-start.28 = (f32[1360]{0:T(1024)}, f32[1360]{0:T(1024)S(1)}, u32[]{:S(2)}) copy-start(f32[1360]{0:T(1024)S(1)} %add_rsqrt_fusion.3) | copy-start | bytes 16324
  151.3 60.4 %collective-permute-start = (bf16[1360,1024]{1,0:T(8,128)(2,1)}, bf16[1360,1024]{1,0:T(8,128)(2,1)}, u32[]{:S(2)}, u32[]{:S(2)}) collective-permute-start(bf16[1360,1024]{1,0:T(8,128)(2,1)} %convolution_convert_fusion.4), channel_id=1, source_target_pairs={{0,1},{1,0},{2,3},{3,2},{4,5},{5,4},{6,7},{7,6},{8,9},{9,8},{10,11... | collective-permute-start | bytes 8355848 | tf_op jit(solution)/shard_map/ppermute | solution.py:29
  243.2 130.2 %collective-permute-start.1 = (bf16[1360,1024]{1,0:T(8,128)(2,1)}, bf16[1360,1024]{1,0:T(8,128)(2,1)}, u32[]{:S(2)}, u32[]{:S(2)}) collective-permute-start(bf16[1360,1024]{1,0:T(8,128)(2,1)} %convolution_convert_fusion.1), channel_id=1, source_target_pairs={{0,1},{1,0},{2,3},{3,2},{4,5},{5,4},{6,7},{7,6},{8,9},{9,8},{10,11... | collective-permute-start | bytes 8355848 | tf_op jit(solution)/shard_map/ppermute | solution.py:29
  271.7 90.7 %collective-permute-start.2 = (bf16[1360,1024]{1,0:T(8,128)(2,1)}, bf16[1360,1024]{1,0:T(8,128)(2,1)}, u32[]{:S(2)}, u32[]{:S(2)}) collective-permute-start(bf16[1360,1024]{1,0:T(8,128)(2,1)} %convolution_convert_fusion), channel_id=1, source_target_pairs={{0,1},{1,0},{2,3},{3,2},{4,5},{5,4},{6,7},{7,6},{8,9},{9,8},{10,11... | collective-permute-start | bytes 8355848 | tf_op jit(solution)/shard_map/ppermute | solution.py:29
  446.9 28.4 %copy-start.13 = (f32[2,680,8]{1,2,0:T(8,128)S(1)}, f32[2,680,8]{1,2,0:T(8,128)}, u32[]{:S(2)}) copy-start(f32[2,680,8]{1,2,0:T(8,128)} %copy-done.12) | copy-start | bytes 130564
  446.9 28.5 %copy-start.31 = (f32[8]{0:T(128)S(1)}, f32[8]{0:T(128)}, u32[]{:S(2)}) copy-start(f32[8]{0:T(128)} %copy-done.30) | copy-start | bytes 100
  542.6 58.7 %collective-permute-start.3 = (bf16[1360,1024]{1,0:T(8,128)(2,1)}, bf16[1360,1024]{1,0:T(8,128)(2,1)}, u32[]{:S(2)}, u32[]{:S(2)}) collective-permute-start(bf16[1360,1024]{1,0:T(8,128)(2,1)} %bitcast_convert_fusion), channel_id=1, source_target_pairs={{0,1},{1,0},{2,3},{3,2},{4,5},{5,4},{6,7},{7,6},{8,9},{9,8},{10,11... | collective-permute-start | bytes 8355848 | tf_op jit(solution)/shard_map/ppermute | solution.py:29
  556.9 44.4 %copy-start.33 = (f32[2,1024]{1,0:T(2,128)S(1)}, f32[2,1024]{1,0:T(2,128)}, u32[]{:S(2)}) copy-start(f32[2,1024]{1,0:T(2,128)} %copy-done.32) | copy-start | bytes 24580
  566.3 38.2 %copy-start.4 = (bf16[1360,1024]{1,0:T(8,128)(2,1)S(1)}, bf16[1360,1024]{1,0:T(8,128)(2,1)}, u32[]{:S(2)}) copy-start(bf16[1360,1024]{1,0:T(8,128)(2,1)} %param.17) | copy-start | bytes 8355844
  566.3 38.2 %copy-start.26 = (f32[1360]{0:T(1024)S(1)}, f32[1360]{0:T(1024)}, u32[]{:S(2)}) copy-start(f32[1360]{0:T(1024)} %copy-done.25) | copy-start | bytes 16324
  566.4 38.2 %copy-start.29 = (f32[1360]{0:T(1024)S(1)}, f32[1360]{0:T(1024)}, u32[]{:S(2)}) copy-start(f32[1360]{0:T(1024)} %copy-done.28) | copy-start | bytes 16324
  626.4 7.2 collective-permute-start.4
  626.4 7.2 collective-permute-start.5
  633.5 100.8 %reduce-scatter.2.cloned.1.call-start = ((), (), s32[]{:S(2)}) async-start(), calls=%async_computation.1 | async-start | bytes 196608 | tf_op jit(solution)/shard_map/reduce_scatter | solution.py:215
  633.6 5.9 collective-permute-start.6
  633.7 5.8 collective-permute-start.7
  639.5 5.8 collective-permute-start.8
  639.5 5.8 collective-permute-start.9
  645.3 5.8 collective-permute-start.10
  645.3 5.9 collective-permute-start.11
  651.1 5.8 collective-permute-start.12
  651.2 5.8 collective-permute-start.13
  657.0 5.8 collective-permute-start.14
  657.0 5.9 collective-permute-start.15
  662.8 5.8 collective-permute-start.16
  662.9 5.8 collective-permute-start.17
  668.6 5.8 collective-permute-start.18
  679.9 280.0 %all-reduce.7.cloned.1.call-start = ((), (), s32[]{:S(2)}) async-start(), calls=%async_computation.3 | async-start | bytes 25165824 | tf_op jit(solution)/shard_map/psum | solution.py:224
  685.2 42.3 %copy-start.24 = (bf16[32,1024]{1,0:T(8,128)(2,1)S(1)}, bf16[32,1024]{1,0:T(8,128)(2,1)}, u32[]{:S(2)}) copy-start(bf16[32,1024]{1,0:T(8,128)(2,1)} %copy-done.23) | copy-start | bytes 196612
  (46 other events, 427.8 us)
Sparse Core Ops, SparseCore 0:
  633.6 87.7 all-reduce.4
  726.6 233.2 all-reduce.6
Sparse Core Ops, SparseCore 1:
  680.0 7.2 reduce-scatter.1
